TPU v7x, 32 devices: a whole 2x2x4 slice. The times are simulated.
32 devices in a mesh: wide: 8 (over y, x, core), narrow: 4 (over z).
Axes of the slice: x: 2, y: 2, z: 4, core: 2. Of those that a mesh axis runs over, the one named last changes fastest.
Arguments:
- tokens: bfloat16 [64, 512, 512], P(('wide', 'narrow')), may hold values from -6 to 6
- seg_ids: int32 [64, 512], P(('wide', 'narrow')), may hold values from 0 to 7, as said below
- positives: int32 [256], replicated, may hold values from 0 to 63
- norm1_gain: bfloat16 [512], replicated, may hold values from 0.5 to 1.5
- w_query: bfloat16 [512, 512], replicated, may hold values from -0.0625 to 0.0625
- w_key: bfloat16 [512, 512], replicated, may hold values from -0.25 to 0.25
- w_value: bfloat16 [512, 512], replicated, may hold values from -0.25 to 0.25
- w_attn_out: bfloat16 [512, 512], replicated, may hold values from -1 to 1
- rel_bias: bfloat16 [32, 8], replicated, may hold values from -4 to 4
- norm2_gain: bfloat16 [512], replicated, may hold values from 0.5 to 1.5
- w_in: bfloat16 [512, 2048], replicated, may hold values from -0.25 to 0.25
- w_ffn_out: bfloat16 [2048, 512], replicated, may hold values from -0.1875 to 0.1875
- w_proj: bfloat16 [512, 512], replicated, may hold values from -0.25 to 0.25
Outputs:
- loss: float32 [], replicated
- tokens_grad: bfloat16 [64, 512, 512], P(('wide', 'narrow'))
- norm1_gain_grad: float32 [512], replicated
- w_query_grad: float32 [512, 512], replicated
- w_key_grad: float32 [512, 512], replicated
- w_value_grad: float32 [512, 512], replicated
- w_attn_out_grad: float32 [512, 512], replicated
- rel_bias_grad: float32 [32, 8], replicated
- norm2_gain_grad: float32 [512], replicated
- w_in_grad: float32 [512, 2048], replicated
- w_ffn_out_grad: float32 [2048, 512], replicated
- w_proj_grad: float32 [512, 512], replicated
Inputs may be any that keep to these rules, and one draw needn't show every extreme that they name: `seg_ids`: each row of the first half holds 8 queries of 64 tokens, numbered 0 to 7 in order. Each row of the second half holds passage 0 and then passage 1, each of 64 to 448 tokens; the first such row has a passage 0 of exactly 448 tokens. `positives`: passages are numbered by row of the second half and then by their number within the row.
All inputs are finite; a program needn't handle non-finite values.
Results may differ from a plain program's by a relative error of at most 0.04.
The roundings to bfloat16 on the way count: a program that leaves them out, or rounds other values in their place, can miss the bound.
Values may be sent and summed in bfloat16 or wider, within the bound.
No kernel may reach another device: no remote copies, remote signals or barrier semaphores. Data moves between devices by JAX's collectives and lax.ppermute only.
A program may use at most 192 MiB of HBM per device.

v0:
```python
import jax
import jax.numpy as jnp
import numpy as np
from jax import lax
from jax.sharding import PartitionSpec as P

NB = 32
MAXD = 128
QLEN = 64
PPR = 2
EPS_NORM = 1e-06
LOGIT_SCALE = 50.0
MASKED = -1e30
HIGHEST = lax.Precision.HIGHEST
F32 = jnp.float32
BF16 = jnp.bfloat16


def bucket_offsets(length):
    offset = np.arange(-(length - 1), length)
    half_count = NB // 2
    exact_span = half_count // 2
    distance = -offset
    bucket = (distance < 0).astype(np.int64) * half_count
    distance = np.abs(distance)
    far_bucket = exact_span + (
        np.log(np.maximum(distance, 1) / exact_span)
        / np.log(MAXD / exact_span)
        * (half_count - exact_span)
    ).astype(np.int64)
    far_bucket = np.minimum(far_bucket, half_count - 1)
    bucket = bucket + np.where(distance < exact_span, distance, far_bucket)
    return bucket.astype(np.int32)


def toeplitz_rows(values, length):
    lead_shape = values.shape[:-1]
    tiled_values = jnp.tile(values, (1,) * len(lead_shape) + (length + 1,))
    start_at = length - 1
    window = tiled_values[..., start_at : start_at + length * (2 * length - 2)]
    return window.reshape(lead_shape + (length, 2 * length - 2))[..., :length]


def contract(left, right, left_dim, right_dim):
    return lax.dot_general(
        left, right, (((left_dim,), (right_dim,)), ((), ())), preferred_element_type=F32
    )


def rms_scale(values):
    return lax.rsqrt(jnp.mean(values * values, axis=-1, keepdims=True) + EPS_NORM)


def norm_back(grad_normed, inputs, scale, gain):
    scaled = grad_normed * gain
    return scale * scaled - inputs * scale**3 * jnp.mean(inputs * scaled, axis=-1, keepdims=True)


def score_block(queries, keys_rows, bias_full, same_seg):
    scores = jnp.einsum("ihd,jhd->hij", queries, keys_rows, preferred_element_type=F32) + bias_full
    return jnp.where(same_seg[None], scores, MASKED)


def local(
    tokens,
    seg_ids,
    positives,
    norm1_gain,
    w_query,
    w_key,
    w_value,
    w_attn_out,
    rel_bias,
    norm2_gain,
    w_in,
    w_ffn_out,
    w_proj,
):
    row_count, length, model_width = tokens.shape
    bucket_count, head_count = rel_bias.shape
    head_size = model_width // head_count
    slot_count = length // QLEN
    linear = lax.axis_index("wide") * lax.axis_size("narrow") + lax.axis_index("narrow")
    is_query = lax.axis_index("wide") < lax.axis_size("wide") // 2
    query_flag = is_query.astype(F32)
    gain_one = norm1_gain.astype(F32)
    gain_two = norm2_gain.astype(F32)
    offset_table = jnp.asarray(bucket_offsets(length))
    bucket_ids = jnp.arange(bucket_count, dtype=jnp.int32)
    offset_onehot = (offset_table[:, None] == bucket_ids[None, :]).astype(F32)
    offset_bias = jnp.dot(offset_onehot, rel_bias.astype(F32), precision=HIGHEST).T
    bias_full = toeplitz_rows(offset_bias, length)
    slot_ids = jnp.arange(slot_count, dtype=jnp.int32)
    stored = []
    embedded_rows = []
    for row_index in range(row_count):
        row_input = tokens[row_index].astype(F32)
        seg_row = seg_ids[row_index]
        scale_one = rms_scale(row_input)
        normed_one = (row_input * scale_one * gain_one).astype(BF16)
        queries = (
            jnp.dot(normed_one, w_query, preferred_element_type=F32)
            .astype(BF16)
            .reshape(length, head_count, head_size)
        )
        keys_rows = (
            jnp.dot(normed_one, w_key, preferred_element_type=F32)
            .astype(BF16)
            .reshape(length, head_count, head_size)
        )
        values_rows = (
            jnp.dot(normed_one, w_value, preferred_element_type=F32)
            .astype(BF16)
            .reshape(length, head_count, head_size)
        )
        same_seg = seg_row[:, None] == seg_row[None, :]
        scores = score_block(queries, keys_rows, bias_full, same_seg)
        row_top = jnp.max(scores, axis=-1, keepdims=True)
        exp_scores = jnp.exp(scores - row_top)
        row_total = jnp.sum(exp_scores, axis=-1, keepdims=True)
        attn_probs = exp_scores / row_total
        log_total = row_top + jnp.log(row_total)
        attn_mixed = jnp.einsum(
            "hij,jhd->ihd", attn_probs.astype(BF16), values_rows, preferred_element_type=F32
        )
        attn_mixed = attn_mixed.reshape(length, model_width).astype(BF16)
        hidden = row_input + jnp.dot(attn_mixed, w_attn_out, preferred_element_type=F32)
        scale_two = rms_scale(hidden)
        normed_two = (hidden * scale_two * gain_two).astype(BF16)
        ffn_inner = jnp.dot(normed_two, w_in, preferred_element_type=F32)
        active = jnp.where(ffn_inner > 0, ffn_inner, 0.0).astype(BF16)
        output = hidden + jnp.dot(active, w_ffn_out, preferred_element_type=F32)
        slot_mask = (seg_row[None, :] == slot_ids[:, None]).astype(F32)
        counts = jnp.maximum(jnp.sum(slot_mask, axis=-1, keepdims=True), 1.0)
        pooled = (jnp.dot(slot_mask, output, precision=HIGHEST) / counts).astype(BF16)
        projected = jnp.dot(pooled, w_proj, preferred_element_type=F32)
        inv_norm = lax.rsqrt(jnp.sum(projected * projected, axis=-1, keepdims=True) + EPS_NORM)
        embedded_rows.append((projected * inv_norm).astype(BF16))
        stored.append(
            (
                row_input,
                same_seg,
                scale_one,
                normed_one,
                queries,
                keys_rows,
                values_rows,
                log_total,
                attn_mixed,
                hidden,
                scale_two,
                normed_two,
                ffn_inner,
                active,
                slot_mask,
                counts,
                pooled,
                projected,
                inv_norm,
            )
        )
    emb_local = jnp.concatenate(embedded_rows, axis=0)
    own_count = row_count * slot_count
    gathered = lax.all_gather(emb_local, ("wide", "narrow"), axis=0, tiled=True)
    half_rows = gathered.shape[0] // (2 * slot_count)
    proj_width = gathered.shape[1]
    passage_all = (
        gathered[half_rows * slot_count :]
        .reshape(half_rows, slot_count, proj_width)[:, :PPR]
        .reshape(half_rows * PPR, proj_width)
    )
    passage_count = half_rows * PPR
    query_start = linear * own_count
    passage_ids = jnp.arange(passage_count, dtype=jnp.int32)
    targets = lax.dynamic_slice_in_dim(positives, query_start, own_count)
    logits = LOGIT_SCALE * contract(emb_local, passage_all, 1, 1)
    row_top = jnp.max(logits, axis=-1, keepdims=True)
    loss_log_total = row_top + jnp.log(jnp.sum(jnp.exp(logits - row_top), axis=-1, keepdims=True))
    pos_hits = (targets[:, None] == passage_ids[None, :]).astype(F32)
    per_query = loss_log_total[:, 0] - jnp.sum(logits * pos_hits, axis=-1)
    weights = (jnp.exp(logits - loss_log_total) - pos_hits).astype(BF16)
    per_query, weights = (per_query, weights)
    loss_part = query_flag * jnp.sum(per_query)
    query_grad = LOGIT_SCALE * jnp.dot(weights, passage_all, preferred_element_type=F32)
    passage_part = LOGIT_SCALE * query_flag * contract(weights, emb_local, 0, 0)
    operand = jnp.concatenate([jnp.zeros_like(passage_part), passage_part], axis=0)
    received = lax.psum_scatter(operand, ("wide", "narrow"), scatter_dimension=0, tiled=True)
    passage_slots = jnp.concatenate(
        [
            received.reshape(row_count, PPR, proj_width),
            jnp.zeros((row_count, slot_count - PPR, proj_width), F32),
        ],
        axis=1,
    ).reshape(own_count, proj_width)
    emb_grad = jnp.where(is_query, query_grad, passage_slots)
    grad_proj = jnp.zeros(w_proj.shape, F32)
    grad_ffn_out = jnp.zeros(w_ffn_out.shape, F32)
    grad_in = jnp.zeros(w_in.shape, F32)
    grad_gain_two = jnp.zeros((model_width,), F32)
    hidden_grads = []
    for row_index in range(row_count):
        (
            row_input,
            same_seg,
            scale_one,
            normed_one,
            queries,
            keys_rows,
            values_rows,
            log_total,
            attn_mixed,
            hidden,
            scale_two,
            normed_two,
            ffn_inner,
            active,
            slot_mask,
            counts,
            pooled,
            projected,
            inv_norm,
        ) = stored[row_index]
        emb_row_grad = emb_grad[row_index * slot_count : (row_index + 1) * slot_count]
        proj_grad = inv_norm * emb_row_grad - projected * inv_norm**3 * jnp.sum(
            emb_row_grad * projected, axis=-1, keepdims=True
        )
        proj_low = proj_grad.astype(BF16)
        grad_proj = grad_proj + contract(pooled, proj_low, 0, 0)
        pooled_grad = contract(proj_low, w_proj, 1, 1)
        out_grad = lax.dot_general(
            slot_mask, pooled_grad / counts, (((0,), (0,)), ((), ())), precision=HIGHEST
        )
        ffn_out_low = out_grad.astype(BF16)
        grad_ffn_out = grad_ffn_out + contract(active, ffn_out_low, 0, 0)
        active_grad = contract(ffn_out_low, w_ffn_out, 1, 1)
        inner_grad = jnp.where(ffn_inner > 0, active_grad, 0.0).astype(BF16)
        grad_in = grad_in + contract(normed_two, inner_grad, 0, 0)
        normed_two_grad = contract(inner_grad, w_in, 1, 1)
        grad_gain_two = grad_gain_two + jnp.sum(normed_two_grad * hidden * scale_two, axis=0)
        hidden_grads.append(out_grad + norm_back(normed_two_grad, hidden, scale_two, gain_two))
    grad_query = jnp.zeros(w_query.shape, F32)
    grad_key = jnp.zeros(w_key.shape, F32)
    grad_value = jnp.zeros(w_value.shape, F32)
    grad_attn_out = jnp.zeros(w_attn_out.shape, F32)
    score_grad_sum = jnp.zeros((head_count, length, length), F32)
    grad_gain_one = jnp.zeros((model_width,), F32)
    token_grads = []
    for row_index in range(row_count):
        (
            row_input,
            same_seg,
            scale_one,
            normed_one,
            queries,
            keys_rows,
            values_rows,
            log_total,
            attn_mixed,
            hidden,
            scale_two,
            normed_two,
            ffn_inner,
            active,
            slot_mask,
            counts,
            pooled,
            projected,
            inv_norm,
        ) = stored[row_index]
        hidden_grad = hidden_grads[row_index]
        attn_low = hidden_grad.astype(BF16)
        grad_attn_out = grad_attn_out + contract(attn_mixed, attn_low, 0, 0)
        mixed_grad = (
            contract(attn_low, w_attn_out, 1, 1).astype(BF16).reshape(length, head_count, head_size)
        )
        attn_probs = jnp.exp(score_block(queries, keys_rows, bias_full, same_seg) - log_total)
        values_grad = (
            jnp.einsum(
                "hij,ihd->jhd", attn_probs.astype(BF16), mixed_grad, preferred_element_type=F32
            )
            .astype(BF16)
            .reshape(length, model_width)
        )
        probs_grad = jnp.einsum("ihd,jhd->hij", mixed_grad, values_rows, preferred_element_type=F32)
        score_grad = (
            attn_probs * (probs_grad - jnp.sum(attn_probs * probs_grad, axis=-1, keepdims=True))
        ).astype(BF16)
        queries_grad = (
            jnp.einsum("hij,jhd->ihd", score_grad, keys_rows, preferred_element_type=F32)
            .astype(BF16)
            .reshape(length, model_width)
        )
        keys_grad = (
            jnp.einsum("hij,ihd->jhd", score_grad, queries, preferred_element_type=F32)
            .astype(BF16)
            .reshape(length, model_width)
        )
        score_grad_sum = score_grad_sum + score_grad.astype(F32)
        grad_query = grad_query + contract(normed_one, queries_grad, 0, 0)
        grad_key = grad_key + contract(normed_one, keys_grad, 0, 0)
        grad_value = grad_value + contract(normed_one, values_grad, 0, 0)
        normed_one_grad = (
            contract(queries_grad, w_query, 1, 1)
            + contract(keys_grad, w_key, 1, 1)
            + contract(values_grad, w_value, 1, 1)
        )
        grad_gain_one = grad_gain_one + jnp.sum(normed_one_grad * row_input * scale_one, axis=0)
        token_grads.append(
            (hidden_grad + norm_back(normed_one_grad, row_input, scale_one, gain_one)).astype(BF16)
        )
    pair_bucket = toeplitz_rows(offset_table[None, :], length)[0]
    pair_onehot = (bucket_ids[:, None] == pair_bucket.reshape(1, length * length)).astype(F32)
    grad_bias = lax.dot_general(
        score_grad_sum.reshape(head_count, length * length),
        pair_onehot,
        (((1,), (1,)), ((), ())),
        precision=HIGHEST,
    )
    sum_query, sum_key, sum_value, sum_attn_out, sum_in, sum_ffn_out, sum_proj = (
        lax.psum_scatter(
            grad_query.reshape(-1), ("wide", "narrow"), scatter_dimension=0, tiled=True
        ),
        lax.psum_scatter(grad_key.reshape(-1), ("wide", "narrow"), scatter_dimension=0, tiled=True),
        lax.psum_scatter(
            grad_value.reshape(-1), ("wide", "narrow"), scatter_dimension=0, tiled=True
        ),
        lax.psum_scatter(
            grad_attn_out.reshape(-1), ("wide", "narrow"), scatter_dimension=0, tiled=True
        ),
        lax.psum_scatter(grad_in.reshape(-1), ("wide", "narrow"), scatter_dimension=0, tiled=True),
        lax.psum_scatter(
            grad_ffn_out.reshape(-1), ("wide", "narrow"), scatter_dimension=0, tiled=True
        ),
        lax.psum_scatter(
            grad_proj.reshape(-1), ("wide", "narrow"), scatter_dimension=0, tiled=True
        ),
    )
    total_query, total_key, total_value, total_attn_out, total_in, total_ffn_out, total_proj = (
        lax.all_gather(
            sum_query.astype(jnp.bfloat16), ("wide", "narrow"), axis=0, tiled=True
        ).astype(sum_query.dtype),
        lax.all_gather(sum_key.astype(jnp.bfloat16), ("wide", "narrow"), axis=0, tiled=True).astype(
            sum_key.dtype
        ),
        lax.all_gather(
            sum_value.astype(jnp.bfloat16), ("wide", "narrow"), axis=0, tiled=True
        ).astype(sum_value.dtype),
        lax.all_gather(
            sum_attn_out.astype(jnp.bfloat16), ("wide", "narrow"), axis=0, tiled=True
        ).astype(sum_attn_out.dtype),
        lax.all_gather(sum_in.astype(jnp.bfloat16), ("wide", "narrow"), axis=0, tiled=True).astype(
            sum_in.dtype
        ),
        lax.all_gather(
            sum_ffn_out.astype(jnp.bfloat16), ("wide", "narrow"), axis=0, tiled=True
        ).astype(sum_ffn_out.dtype),
        lax.all_gather(
            sum_proj.astype(jnp.bfloat16), ("wide", "narrow"), axis=0, tiled=True
        ).astype(sum_proj.dtype),
    )
    loss_total, total_gain_one, total_gain_two, total_bias = lax.psum(
        (loss_part, grad_gain_one, grad_gain_two, grad_bias), ("wide", "narrow")
    )
    tokens_grad = jnp.stack(token_grads, axis=0)
    return (
        loss_total,
        tokens_grad,
        total_gain_one,
        total_query.reshape(w_query.shape),
        total_key.reshape(w_key.shape),
        total_value.reshape(w_value.shape),
        total_attn_out.reshape(w_attn_out.shape),
        total_bias.T,
        total_gain_two,
        total_in.reshape(w_in.shape),
        total_ffn_out.reshape(w_ffn_out.shape),
        total_proj.reshape(w_proj.shape),
    )


def solution(mesh):
    in_specs = (
        P(("wide", "narrow"), None, None),
        P(("wide", "narrow"), None),
        P(),
        P(),
        P(),
        P(),
        P(),
        P(),
        P(),
        P(),
        P(),
        P(),
        P(),
    )
    out_specs = (
        P(),
        P(("wide", "narrow"), None, None),
        P(),
        P(),
        P(),
        P(),
        P(),
        P(),
        P(),
        P(),
        P(),
        P(),
    )
    return jax.shard_map(local, mesh=mesh, in_specs=in_specs, out_specs=out_specs, check_vma=False)
```

profile of v0, /device:TPU:0, one launch (start us, length us, event | category | flops | bytes accessed | tf_op | source)
XLA Modules:
  0.0 1305.5 jit_solution(8156129899407925416)
XLA Ops:
  15.2 2.4 convolution_convert_fusion.10
  17.6 2.4 convolution_convert_fusion.9
  25.7 8.0 tile.8
  33.7 211.9 %while.1 = (u32[]{:T(128)}, f32[8,513,1023]{2,1,0:T(8,128)}, f32[4198392]{0:T(1024)}, u32[]{}, u32[]{}, /*index=5*/u32[]{}, u32[]{}) while((u32[]{:T(128)}, f32[8,513,1023]{2,1,0:T(8,128)}, f32[4198392]{0:T(1024)}, u32[]{}, u32[]{}, /*index=5*/u32[]{}, u32[]{}) %tuple.60), condition=%wide.cond, body=%wide.body.sunk | while | flops 9 | bytes 12595357
  34.2 3.2 constant_dynamic-slice_fusion.3
  37.4 4.2 reshape.518
  41.6 19.0 %dynamic-update-slice.2 = f32[4198392]{0:T(1024)} dynamic-update-slice(f32[4198392]{0:T(1024)} %get-tuple-element.177, f32[524799]{0:T(1024)} %reshape.518, u32[]{:T(128)S(6)} %add.320) | dynamic-update-slice | bytes 4198396
  60.6 3.2 constant_dynamic-slice_fusion.3
  63.8 4.2 reshape.518
  68.0 19.0 %dynamic-update-slice.2 = f32[4198392]{0:T(1024)} dynamic-update-slice(f32[4198392]{0:T(1024)} %get-tuple-element.177, f32[524799]{0:T(1024)} %reshape.518, u32[]{:T(128)S(6)} %add.320) | dynamic-update-slice | bytes 4198396
  87.0 3.2 constant_dynamic-slice_fusion.3
  90.2 4.2 reshape.518
  94.4 19.0 %dynamic-update-slice.2 = f32[4198392]{0:T(1024)} dynamic-update-slice(f32[4198392]{0:T(1024)} %get-tuple-element.177, f32[524799]{0:T(1024)} %reshape.518, u32[]{:T(128)S(6)} %add.320) | dynamic-update-slice | bytes 4198396
  113.4 3.2 constant_dynamic-slice_fusion.3
  116.6 4.2 reshape.518
  120.8 19.0 %dynamic-update-slice.2 = f32[4198392]{0:T(1024)} dynamic-update-slice(f32[4198392]{0:T(1024)} %get-tuple-element.177, f32[524799]{0:T(1024)} %reshape.518, u32[]{:T(128)S(6)} %add.320) | dynamic-update-slice | bytes 4198396
  139.9 3.2 constant_dynamic-slice_fusion.3
  143.0 4.2 reshape.518
  147.3 19.0 %dynamic-update-slice.2 = f32[4198392]{0:T(1024)} dynamic-update-slice(f32[4198392]{0:T(1024)} %get-tuple-element.177, f32[524799]{0:T(1024)} %reshape.518, u32[]{:T(128)S(6)} %add.320) | dynamic-update-slice | bytes 4198396
  166.3 3.2 constant_dynamic-slice_fusion.3
  169.5 4.2 reshape.518
  173.7 19.1 %dynamic-update-slice.2 = f32[4198392]{0:T(1024)} dynamic-update-slice(f32[4198392]{0:T(1024)} %get-tuple-element.177, f32[524799]{0:T(1024)} %reshape.518, u32[]{:T(128)S(6)} %add.320) | dynamic-update-slice | bytes 4198396
  192.8 3.2 constant_dynamic-slice_fusion.3
  196.0 4.2 reshape.518
  200.2 19.1 %dynamic-update-slice.2 = f32[4198392]{0:T(1024)} dynamic-update-slice(f32[4198392]{0:T(1024)} %get-tuple-element.177, f32[524799]{0:T(1024)} %reshape.518, u32[]{:T(128)S(6)} %add.320) | dynamic-update-slice | bytes 4198396
  219.3 3.2 constant_dynamic-slice_fusion.3
  222.5 4.2 reshape.518
  226.7 18.9 %dynamic-update-slice.2 = f32[4198392]{0:T(1024)} dynamic-update-slice(f32[4198392]{0:T(1024)} %get-tuple-element.177, f32[524799]{0:T(1024)} %reshape.518, u32[]{:T(128)S(6)} %add.320) | dynamic-update-slice | bytes 4198396
  245.6 20.6 %tile.18 = f32[8,524799]{1,0:T(8,128)} reshape(f32[4198392]{0:T(1024)} %get-tuple-element.64) | data formatting | bytes 33587136 | tf_op jit(solution)/shard_map/tile | solution.py:38
  266.2 12.9 slice.48
  279.0 13.9 %reshape.515 = f32[4186112]{0:T(1024)} reshape(f32[8,523264]{1,0:T(8,128)} %slice.48) | data formatting | bytes 33488896
  292.9 18.2 %reshape.451 = f32[8,512,1022]{2,1,0:T(8,128)} reshape(f32[4186112]{0:T(1024)} %reshape.515) | data formatting | bytes 33488896 | tf_op jit(solution)/shard_map/reshape | solution.py:41
  311.1 7.6 slice.49
  318.8 9.3 copy.147
  328.0 5.3 fusion.118
  334.6 2.7 copy-done.2
  357.9 73.9 %all_gather.24 = bf16[512,512]{1,0:T(8,128)(2,1)S(1)} all-gather(bf16[16,512]{1,0:T(8,128)(2,1)S(1)} %pad_maximum_fusion.1), channel_id=1, replica_groups=mesh['wide'=8,'narrow'=4] {'wide','narrow'}, dimensions={0}, use_global_device_ids=true | all-gather | bytes 540672 | tf_op jit(solution)/shard_map/all_gather | solution.py:164
  435.8 6.2 tile.20
  442.0 24.4 %slice_reduce_fusion = s32[523264]{0:T(1024)} fusion(s32[1,524799]{1,0:T(1,128)} %tile.20), kind=kLoop, calls=%fused_computation.36 | loop fusion | bytes 4186112 | tf_op jit(solution)/shard_map/slice | solution.py:40
  466.4 4.5 reshape.480
  474.1 83.0 %all-reduce.14.cloned.1.call-done = f32[128,512]{1,0:T(8,128)} async-done(((f32[128,512]{1,0:T(8,128)}), f32[128,512]{1,0:T(8,128)}) %all-reduce.14.cloned.1.call-update) | async-done | bytes 262160
  562.5 2.5 copy.109
  565.1 5.9 fusion.7
  571.0 3.2 fusion.70
  576.1 2.5 copy.117
  578.6 4.4 fusion.9
  590.8 3.3 fusion.97
  597.0 5.1 multiply_reduce_fusion
  603.6 5.1 multiply_reduce_fusion.1
  608.7 18.7 %convert_add_fusion = (f32[8,512,512]{1,2,0:T(8,128)}, bf16[8,512,512]{1,2,0:T(8,128)(2,1)}, bf16[8,512,512]{1,2,0:T(8,128)(2,1)}) fusion(f32[8,512,512]{1,2,0:T(8,128)} %get-tuple-element.141, f32[8,512]{1,0:T(8,128)S(1)} %get-tuple-element.140, f32[8,512,512]{1,2,0:T(8,128)} %copy-done.2, f32[8,512]{1,0:T(8,128)S(1)} %get-tuple-element.147, ...), kind=kLoop, calls=%fused_computation.3 | loop fusion | flops 23068672 | bytes 50397184 | tf_op jit(solution)/shard_map/add | solution.py:298
  627.4 4.7 convolution_convert_fusion.2
  642.7 3.1 copy.156
  649.8 2.9 copy.155
  655.0 9.3 copy.124
  664.3 8.3 copy.154
  678.6 15.9 %fusion = f32[32,8]{0,1:T(8,128)S(1)} fusion(f32[8,262144]{1,0:T(8,128)S(1)} %bitcast.251, s32[262144]{0:T(1024)S(1)} %bitcast.285), kind=kOutput, calls=%fused_computation.1 | convolution fusion | flops 813694976 | bytes 9438208 | tf_op jit(solution)/shard_map/dot_general | solution.py:313
  696.3 230.0 %all-reduce.15 = (bf16[262144]{0:T(1024)(128)(2,1)}, bf16[262144]{0:T(1024)(128)(2,1)}, bf16[262144]{0:T(1024)(128)(2,1)}, bf16[262144]{0:T(1024)(128)(2,1)}, bf...) all-reduce(f32[262144]{0:T(1024)} %bitcast.272, ...), channel_id=3, replica_groups=mesh['wide'=8,'narrow'=4] {'wide','narrow'}, use_global_device_ids=true, to_apply=%region_29.30.clone | all-reduce | flops 3409153 | bytes 20457480
  936.6 70.3 %all_gather.25 = bf16[262144]{0:T(1024)(128)(2,1)S(1)} all-gather(bf16[8192]{0:T(1024)(128)(2,1)S(1)} %dynamic-slice.23), channel_id=1, replica_groups=mesh['wide'=8,'narrow'=4] {'wide','narrow'}, dimensions={0}, use_global_device_ids=true | all-gather | bytes 540672 | tf_op jit(solution)/shard_map/all_gather | solution.py:339
  1008.1 69.5 %all_gather.26 = bf16[262144]{0:T(1024)(128)(2,1)S(1)} all-gather(bf16[8192]{0:T(1024)(128)(2,1)S(1)} %dynamic-slice.22), channel_id=1, replica_groups=mesh['wide'=8,'narrow'=4] {'wide','narrow'}, dimensions={0}, use_global_device_ids=true | all-gather | bytes 540672 | tf_op jit(solution)/shard_map/all_gather | solution.py:342
  1078.9 69.3 %all_gather.27 = bf16[262144]{0:T(1024)(128)(2,1)S(1)} all-gather(bf16[8192]{0:T(1024)(128)(2,1)S(1)} %dynamic-slice.21), channel_id=1, replica_groups=mesh['wide'=8,'narrow'=4] {'wide','narrow'}, dimensions={0}, use_global_device_ids=true | all-gather | bytes 540672 | tf_op jit(solution)/shard_map/all_gather | solution.py:345
  1149.4 68.1 %all_gather.28 = bf16[262144]{0:T(1024)(128)(2,1)S(1)} all-gather(bf16[8192]{0:T(1024)(128)(2,1)S(1)} %dynamic-slice.20), channel_id=1, replica_groups=mesh['wide'=8,'narrow'=4] {'wide','narrow'}, dimensions={0}, use_global_device_ids=true | all-gather | bytes 540672 | tf_op jit(solution)/shard_map/all_gather | solution.py:348
  1218.8 69.2 %all_gather.31 = bf16[262144]{0:T(1024)(128)(2,1)S(1)} all-gather(bf16[8192]{0:T(1024)(128)(2,1)S(1)} %dynamic-slice.19), channel_id=1, replica_groups=mesh['wide'=8,'narrow'=4] {'wide','narrow'}, dimensions={0}, use_global_device_ids=true | all-gather | bytes 540672 | tf_op jit(solution)/shard_map/all_gather | solution.py:357
  1289.2 4.6 reshape.501
  1293.9 4.6 reshape.503
  (287 shorter events, 101.5 us)
Async XLA Ops:
  7.2 341.4 %copy-start = (bf16[512,2048]{1,0:T(8,128)(2,1)S(1)}, bf16[512,2048]{1,0:T(8,128)(2,1)}, u32[]{:S(2)}) copy-start(bf16[512,2048]{1,0:T(8,128)(2,1)} %param.24) | copy-start | bytes 6291460
  7.2 550.0 %all-reduce.14.cloned.1.call-start = ((), (), s32[]{:S(2)}) async-start(), calls=%async_computation.2 | async-start | bytes 524288
  10.2 13.9 %copy-start.61 = (f32[512]{0:T(512)}, f32[512]{0:T(512)S(1)}, u32[]{:S(2)}) copy-start(f32[512]{0:T(512)S(1)} %convert_element_type.250) | copy-start | bytes 6148
  13.2 10.8 copy-start.63
  14.5 5.5 copy-start.49
  14.5 6.9 copy-start.52
  14.6 8.0 copy-start.54
  15.2 8.8 copy-start.65
  20.0 5.4 copy-start.70
  20.0 5.4 copy-start.69
  20.0 5.4 copy-start.71
  333.3 3.9 copy-start.2
  333.3 3.9 copy-start.59
  334.6 4.8 slice-start.4
  337.2 3.9 slice-start.5
  337.2 3.9 copy-start.40
  337.2 3.9 copy-start.42
  338.8 4.1 copy-start.45
  339.3 15.6 %copy-start.11 = (f32[512,512]{0,1:T(8,128)}, f32[512,512]{0,1:T(8,128)S(1)}, u32[]{:S(2)}) copy-start(f32[512,512]{0,1:T(8,128)S(1)} %get-tuple-element.132) | copy-start | bytes 3145732
  342.9 3.2 copy-start.3
  342.9 3.2 copy-start.57
  348.2 3.3 copy-start.15
  350.2 3.0 copy-start.20
  355.0 77.3 %copy-start.72 = (s32[256]{0:T(256)S(1)}, s32[256]{0:T(256)}, u32[]{:S(2)}) copy-start(s32[256]{0:T(256)} %param.16) | copy-start | bytes 3076
  434.1 855.1 %all-gather.3.cloned.1.call-start = ((), (), s32[]{:S(2)}) async-start(), calls=%async_computation | async-start | bytes 2162688 | tf_op jit(solution)/shard_map/all_gather | solution.py:351
  565.1 5.9 copy-start.5
  565.1 5.9 copy-start.17
  571.0 3.2 copy-start.21
  583.1 4.7 copy-start.22
  583.1 3.0 copy-start.24
  587.9 2.5 copy-start.26
  587.9 6.9 slice-start
  590.3 4.4 slice-start.1
  594.8 7.3 slice-start.2
  597.0 5.1 slice-start.3
  603.6 49.2 %copy-start.27 = (bf16[8,64,512]{2,1,0:T(8,128)(2,1)}, bf16[8,64,512]{2,1,0:T(8,128)(2,1)S(1)}, u32[]{:S(2)}) copy-start(bf16[8,64,512]{2,1,0:T(8,128)(2,1)S(1)} %fusion.35) | copy-start | bytes 1572868
  627.4 4.8 copy-start.9
  627.4 4.8 copy-start.44
  627.4 6.4 copy-start.8
  627.4 6.4 copy-start.43
  632.2 3.8 copy-start.41
  633.8 3.0 copy-start.62
  633.8 3.0 copy-start.66
  636.0 2.3 copy-start.50
  636.0 3.7 copy-start.38
  636.0 5.3 copy-start.18
  636.8 4.5 copy-start.7
  636.9 4.5 copy-start.13
  642.7 3.2 copy-start.34
  642.7 3.2 copy-start.46
  642.7 4.9 copy-start.23
  645.8 2.6 copy-start.14
  649.8 3.5 copy-start.32
  649.8 3.5 copy-start.64
  664.3 8.4 copy-start.30
  664.3 8.9 copy-start.29
  672.6 2.3 copy-start.31
  672.7 2.3 copy-start.51
  678.5 16.0 %copy-start.19 = (f32[512,512]{0,1:T(8,128)}, f32[512,512]{0,1:T(8,128)S(1)}, u32[]{:S(2)}) copy-start(f32[512,512]{0,1:T(8,128)S(1)} %convolution_add_fusion.2) | copy-start | bytes 3145732
  678.6 16.0 %copy-start.33 = (bf16[8,64,512]{2,1,0:T(8,128)(2,1)S(1)}, bf16[8,64,512]{2,1,0:T(8,128)(2,1)}, u32[]{:S(2)}) copy-start(bf16[8,64,512]{2,1,0:T(8,128)(2,1)} %fusion.38) | copy-start | bytes 1572868
  696.3 233.1 %copy-start.67 = (f32[512]{0:T(512)S(1)}, f32[512]{0:T(512)}, u32[]{:S(2)}) copy-start(f32[512]{0:T(512)} %get-tuple-element.109) | copy-start | bytes 6148
  696.3 233.1 %copy-start.68 = (f32[512]{0:T(512)S(1)}, f32[512]{0:T(512)}, u32[]{:S(2)}) copy-start(f32[512]{0:T(512)} %get-tuple-element.107) | copy-start | bytes 6148
  927.9 366.0 %all-gather.5.cloned.1.call-start = ((), (), s32[]{:S(2)}) async-start(), calls=%async_computation.1 | async-start | bytes 2162688 | tf_op jit(solution)/shard_map/all_gather | solution.py:354
  1289.2 9.3 copy-start.1
  (18 other events, 33.3 us)
Sparse Core Ops, SparseCore 0:
  434.2 122.8 all-reduce.13
  928.0 55.0 all-gather.2
  986.0 55.6 all-gather.4
where the time goes:
time: 1320 us; the launch traced here: 1310 us
  blocking collectives  650 us (49%)
  local copies, waits for them, and re-layouts  417 us (32%)
  matrix products  110 us (8%)
  waiting for transfers between devices  83.1 us (6%)
  other arithmetic  28.6 us (2%)
  between operations  15.9 us (1%)
    unnamed x205, local copies, waits for them, and re-layouts  279 us
    unnamed x1, blocking collectives  230 us
    unnamed x4, waiting for transfers between devices  83.1 us
    all_gather x1, blocking collectives, local(): gathered = lax.all_gather(emb_local, ('wide', 'narrow'), axis=0, tiled=True)  73.9 us
    all_gather x1, blocking collectives, local(): lax.all_gather(sum_query.astype(jnp.bfloat16), ('wide', 'narrow'), axis=0...  70.3 us
    all_gather x1, blocking collectives, local(): lax.all_gather(sum_key.astype(jnp.bfloat16), ('wide', 'narrow'), axis=0,...  69.5 us
    all_gather x1, blocking collectives, local(): lax.all_gather(sum_value.astype(jnp.bfloat16), ('wide', 'narrow'), axis=0...  69.3 us
    all_gather x1, blocking collectives, local(): lax.all_gather(sum_proj.astype(jnp.bfloat16), ('wide', 'narrow'), axis=0,...  69.2 us
  transfers between devices with their start and end apart: 3, of which 1 were waited for; matrix products, arithmetic and copies ran while one was open for 5% of the time, Pallas kernels for 0%

commit v1 on v0

--- a/solution.py
+++ b/solution.py
@@ -336,8 +336,14 @@
         ),
     )
     total_query, total_key, total_value, total_attn_out, total_in, total_ffn_out, total_proj = (
-        lax.all_gather(
-            sum_query.astype(jnp.bfloat16), ("wide", "narrow"), axis=0, tiled=True
+        jnp.concatenate(
+            lax.all_to_all(
+                jnp.stack([sum_query.astype(jnp.bfloat16)] * lax.axis_size(("wide", "narrow"))),
+                ("wide", "narrow"),
+                0,
+                0,
+            ),
+            axis=0,
         ).astype(sum_query.dtype),
         lax.all_gather(sum_key.astype(jnp.bfloat16), ("wide", "narrow"), axis=0, tiled=True).astype(
             sum_key.dtype

time: 1320 us -> 1280 us (0.970)
  blocking collectives: 650 us -> 592 us
    all_gather x1 -> x0, blocking collectives: 70.3 us -> none  [local(): lax.all_gather(sum_query.astype(jnp.bfloat16), ('wide', 'narrow'), axis=0...]
    unnamed x205 -> x207, local copies, waits for them, and re-layouts: 279 us -> 281 us
  transfers between devices with their start and end apart: 3 -> 4, of which waited for: 1 -> 1; matrix products, arithmetic and copies ran while one was open for 5% -> 5% of each run, Pallas kernels for 0% -> 0%
where the time goes in v1:
time: 1280 us; the launch traced here: 1260 us
  blocking collectives  592 us (46%)
  local copies, waits for them, and re-layouts  420 us (33%)
  matrix products  110 us (9%)
  waiting for transfers between devices  83.2 us (6%)
  other arithmetic  35.4 us (3%)
  between operations  15.7 us (1%)
    unnamed x207, local copies, waits for them, and re-layouts  281 us
    unnamed x1, blocking collectives  230 us
    unnamed x4, waiting for transfers between devices  83.2 us
    all_gather x1, blocking collectives, local(): lax.all_gather(sum_key.astype(jnp.bfloat16), ('wide', 'narrow'), axis=0,...  81.2 us
    all_gather x1, blocking collectives, local(): gathered = lax.all_gather(emb_local, ('wide', 'narrow'), axis=0, tiled=True)  73.9 us
    all_gather x1, blocking collectives, local(): lax.all_gather(sum_attn_out.astype(jnp.bfloat16), ('wide', 'narrow'), axi...  69.2 us
    all_gather x1, blocking collectives, local(): lax.all_gather(sum_proj.astype(jnp.bfloat16), ('wide', 'narrow'), axis=0,...  69 us
    all_gather x1, blocking collectives, local(): lax.all_gather(sum_value.astype(jnp.bfloat16), ('wide', 'narrow'), axis=0...  68.2 us
  transfers between devices with their start and end apart: 4, of which 1 were waited for; matrix products, arithmetic and copies ran while one was open for 5% of the time, Pallas kernels for 0%

profile of v1, /device:TPU:0, one launch (start us, length us, event | category | flops | bytes accessed | tf_op | source)
XLA Modules:
  0.0 1259.6 jit_solution(4184445287538813280)
XLA Ops:
  25.7 8.0 tile.8
  33.7 212.0 %while.1 = (u32[]{:T(128)}, f32[8,513,1023]{2,1,0:T(8,128)}, f32[4198392]{0:T(1024)}, u32[]{}, u32[]{}, /*index=5*/u32[]{}, u32[]{}) while((u32[]{:T(128)}, f32[8,513,1023]{2,1,0:T(8,128)}, f32[4198392]{0:T(1024)}, u32[]{}, u32[]{}, /*index=5*/u32[]{}, u32[]{}) %tuple.60), condition=%wide.cond, body=%wide.body.sunk | while | flops 9 | bytes 12595357
  34.2 3.2 constant_dynamic-slice_fusion.3
  37.4 4.2 reshape.525
  41.6 19.0 %dynamic-update-slice.2 = f32[4198392]{0:T(1024)} dynamic-update-slice(f32[4198392]{0:T(1024)} %get-tuple-element.177, f32[524799]{0:T(1024)} %reshape.525, u32[]{:T(128)S(6)} %add.322) | dynamic-update-slice | bytes 4198396
  60.6 3.2 constant_dynamic-slice_fusion.3
  63.8 4.2 reshape.525
  68.0 19.0 %dynamic-update-slice.2 = f32[4198392]{0:T(1024)} dynamic-update-slice(f32[4198392]{0:T(1024)} %get-tuple-element.177, f32[524799]{0:T(1024)} %reshape.525, u32[]{:T(128)S(6)} %add.322) | dynamic-update-slice | bytes 4198396
  87.0 3.2 constant_dynamic-slice_fusion.3
  90.2 4.2 reshape.525
  94.5 19.0 %dynamic-update-slice.2 = f32[4198392]{0:T(1024)} dynamic-update-slice(f32[4198392]{0:T(1024)} %get-tuple-element.177, f32[524799]{0:T(1024)} %reshape.525, u32[]{:T(128)S(6)} %add.322) | dynamic-update-slice | bytes 4198396
  113.4 3.2 constant_dynamic-slice_fusion.3
  116.6 4.2 reshape.525
  120.8 19.0 %dynamic-update-slice.2 = f32[4198392]{0:T(1024)} dynamic-update-slice(f32[4198392]{0:T(1024)} %get-tuple-element.177, f32[524799]{0:T(1024)} %reshape.525, u32[]{:T(128)S(6)} %add.322) | dynamic-update-slice | bytes 4198396
  139.9 3.2 constant_dynamic-slice_fusion.3
  143.1 4.2 reshape.525
  147.3 19.0 %dynamic-update-slice.2 = f32[4198392]{0:T(1024)} dynamic-update-slice(f32[4198392]{0:T(1024)} %get-tuple-element.177, f32[524799]{0:T(1024)} %reshape.525, u32[]{:T(128)S(6)} %add.322) | dynamic-update-slice | bytes 4198396
  166.3 3.2 constant_dynamic-slice_fusion.3
  169.5 4.2 reshape.525
  173.8 19.1 %dynamic-update-slice.2 = f32[4198392]{0:T(1024)} dynamic-update-slice(f32[4198392]{0:T(1024)} %get-tuple-element.177, f32[524799]{0:T(1024)} %reshape.525, u32[]{:T(128)S(6)} %add.322) | dynamic-update-slice | bytes 4198396
  192.8 3.2 constant_dynamic-slice_fusion.3
  196.0 4.2 reshape.525
  200.3 19.1 %dynamic-update-slice.2 = f32[4198392]{0:T(1024)} dynamic-update-slice(f32[4198392]{0:T(1024)} %get-tuple-element.177, f32[524799]{0:T(1024)} %reshape.525, u32[]{:T(128)S(6)} %add.322) | dynamic-update-slice | bytes 4198396
  219.3 3.2 constant_dynamic-slice_fusion.3
  222.5 4.2 reshape.525
  226.8 18.9 %dynamic-update-slice.2 = f32[4198392]{0:T(1024)} dynamic-update-slice(f32[4198392]{0:T(1024)} %get-tuple-element.177, f32[524799]{0:T(1024)} %reshape.525, u32[]{:T(128)S(6)} %add.322) | dynamic-update-slice | bytes 4198396
  245.7 20.6 %tile.18 = f32[8,524799]{1,0:T(8,128)} reshape(f32[4198392]{0:T(1024)} %get-tuple-element.64) | data formatting | bytes 33587136 | tf_op jit(solution)/shard_map/tile | solution.py:38
  266.2 12.9 %slice.48 = f32[8,523264]{1,0:T(8,128)} slice(f32[8,524799]{1,0:T(8,128)} %tile.18), slice={[0:8], [511:523775]} | slice | bytes 33488896 | tf_op jit(solution)/shard_map/slice | solution.py:40
  279.1 13.9 %reshape.520 = f32[4186112]{0:T(1024)} reshape(f32[8,523264]{1,0:T(8,128)} %slice.48) | data formatting | bytes 33488896
  293.0 18.2 %reshape.458 = f32[8,512,1022]{2,1,0:T(8,128)} reshape(f32[4186112]{0:T(1024)} %reshape.520) | data formatting | bytes 33488896 | tf_op jit(solution)/shard_map/reshape | solution.py:41
  311.2 7.6 slice.49
  318.8 9.3 copy.147
  328.1 5.3 fusion.118
  334.6 2.7 copy-done.2
  358.0 73.9 %all_gather.21 = bf16[512,512]{1,0:T(8,128)(2,1)S(1)} all-gather(bf16[16,512]{1,0:T(8,128)(2,1)S(1)} %pad_maximum_fusion.1), channel_id=1, replica_groups=mesh['wide'=8,'narrow'=4] {'wide','narrow'}, dimensions={0}, use_global_device_ids=true | all-gather | bytes 540672 | tf_op jit(solution)/shard_map/all_gather | solution.py:164
  435.8 6.2 tile.20
  442.1 24.4 %slice_reduce_fusion = s32[523264]{0:T(1024)} fusion(s32[1,524799]{1,0:T(1,128)} %tile.20), kind=kLoop, calls=%fused_computation.36 | loop fusion | bytes 4186112 | tf_op jit(solution)/shard_map/slice | solution.py:40
  466.4 4.5 reshape.485
  474.1 83.2 %all-reduce.14.cloned.1.call-done = f32[128,512]{1,0:T(8,128)} async-done(((f32[128,512]{1,0:T(8,128)}), f32[128,512]{1,0:T(8,128)}) %all-reduce.14.cloned.1.call-update) | async-done | bytes 262160
  562.7 2.5 copy.109
  565.2 5.9 fusion.7
  571.1 3.2 fusion.70
  576.2 2.5 copy.117
  578.8 4.4 fusion.9
  590.9 3.3 fusion.97
  597.2 5.1 multiply_reduce_fusion
  603.7 5.1 multiply_reduce_fusion.1
  608.8 18.7 %convert_add_fusion = (f32[8,512,512]{1,2,0:T(8,128)}, bf16[8,512,512]{1,2,0:T(8,128)(2,1)}, bf16[8,512,512]{1,2,0:T(8,128)(2,1)}) fusion(f32[8,512,512]{1,2,0:T(8,128)} %get-tuple-element.141, f32[8,512]{1,0:T(8,128)S(1)} %get-tuple-element.140, f32[8,512,512]{1,2,0:T(8,128)} %copy-done.2, f32[8,512]{1,0:T(8,128)S(1)} %get-tuple-element.147, ...), kind=kLoop, calls=%fused_computation.3 | loop fusion | flops 23068672 | bytes 50397184 | tf_op jit(solution)/shard_map/add | solution.py:298
  627.6 4.7 convolution_convert_fusion.2
  642.8 3.1 copy.156
  649.9 2.9 copy.155
  655.1 9.3 copy.124
  664.5 8.3 copy.154
  678.7 15.9 %fusion = f32[32,8]{0,1:T(8,128)S(1)} fusion(f32[8,262144]{1,0:T(8,128)S(1)} %bitcast.251, s32[262144]{0:T(1024)S(1)} %bitcast.285), kind=kOutput, calls=%fused_computation.1 | convolution fusion | flops 813694976 | bytes 9438208 | tf_op jit(solution)/shard_map/dot_general | solution.py:313
  696.5 230.2 %all-reduce.15 = (bf16[262144]{0:T(1024)(128)(2,1)}, bf16[262144]{0:T(1024)(128)(2,1)}, bf16[262144]{0:T(1024)(128)(2,1)}, bf16[1048576]{0:T(1024)(128)(2,1)}, b...) all-reduce(f32[262144]{0:T(1024)} %bitcast.271, ...), channel_id=4, replica_groups=mesh['wide'=8,'narrow'=4] {'wide','narrow'}, use_global_device_ids=true, to_apply=%region_30.31.clone | all-reduce | flops 3409153 | bytes 20457480
  938.3 3.8 reduce.6
  943.3 2.9 all-to-all-start
  946.2 81.2 %all_gather.22 = bf16[262144]{0:T(1024)(128)(2,1)S(1)} all-gather(bf16[8192]{0:T(1024)(128)(2,1)S(1)} %dynamic-slice.22), channel_id=1, replica_groups=mesh['wide'=8,'narrow'=4] {'wide','narrow'}, dimensions={0}, use_global_device_ids=true | all-gather | bytes 540672 | tf_op jit(solution)/shard_map/all_gather | solution.py:348
  1028.7 68.2 %all_gather.23 = bf16[262144]{0:T(1024)(128)(2,1)S(1)} all-gather(bf16[8192]{0:T(1024)(128)(2,1)S(1)} %dynamic-slice.21), channel_id=1, replica_groups=mesh['wide'=8,'narrow'=4] {'wide','narrow'}, dimensions={0}, use_global_device_ids=true | all-gather | bytes 540672 | tf_op jit(solution)/shard_map/all_gather | solution.py:351
  1098.1 69.2 %all_gather.24 = bf16[262144]{0:T(1024)(128)(2,1)S(1)} all-gather(bf16[8192]{0:T(1024)(128)(2,1)S(1)} %dynamic-slice.20), channel_id=1, replica_groups=mesh['wide'=8,'narrow'=4] {'wide','narrow'}, dimensions={0}, use_global_device_ids=true | all-gather | bytes 540672 | tf_op jit(solution)/shard_map/all_gather | solution.py:354
  1168.6 69.0 %all_gather.27 = bf16[262144]{0:T(1024)(128)(2,1)S(1)} all-gather(bf16[8192]{0:T(1024)(128)(2,1)S(1)} %dynamic-slice.19), channel_id=1, replica_groups=mesh['wide'=8,'narrow'=4] {'wide','narrow'}, dimensions={0}, use_global_device_ids=true | all-gather | bytes 540672 | tf_op jit(solution)/shard_map/all_gather | solution.py:363
  1239.4 3.0 convert_reduce_fusion
  1243.6 4.6 reshape.505
  1248.2 4.6 reshape.507
  (294 shorter events, 109.3 us)
Async XLA Ops:
  7.2 341.4 %copy-start = (bf16[512,2048]{1,0:T(8,128)(2,1)S(1)}, bf16[512,2048]{1,0:T(8,128)(2,1)}, u32[]{:S(2)}) copy-start(bf16[512,2048]{1,0:T(8,128)(2,1)} %param.24) | copy-start | bytes 6291460
  7.2 550.1 %all-reduce.14.cloned.1.call-start = ((), (), s32[]{:S(2)}) async-start(), calls=%async_computation.3 | async-start | bytes 524288
  10.2 13.8 %copy-start.61 = (f32[512]{0:T(512)}, f32[512]{0:T(512)S(1)}, u32[]{:S(2)}) copy-start(f32[512]{0:T(512)S(1)} %convert_element_type.256) | copy-start | bytes 6148
  13.2 10.8 copy-start.63
  14.4 5.5 copy-start.49
  14.5 6.9 copy-start.52
  14.6 8.0 copy-start.54
  15.2 8.8 copy-start.65
  20.0 5.3 copy-start.70
  20.0 5.3 copy-start.69
  20.0 5.4 copy-start.71
  333.4 3.9 copy-start.2
  333.4 3.9 copy-start.59
  334.6 4.8 slice-start.4
  337.3 3.9 slice-start.5
  337.3 3.9 copy-start.40
  337.3 3.9 copy-start.42
  338.8 4.1 copy-start.45
  339.4 15.6 %copy-start.11 = (f32[512,512]{0,1:T(8,128)}, f32[512,512]{0,1:T(8,128)S(1)}, u32[]{:S(2)}) copy-start(f32[512,512]{0,1:T(8,128)S(1)} %get-tuple-element.132) | copy-start | bytes 3145732
  343.0 3.2 copy-start.3
  343.0 3.2 copy-start.57
  348.3 3.3 copy-start.15
  350.3 3.0 copy-start.20
  355.0 77.3 %copy-start.72 = (s32[256]{0:T(256)S(1)}, s32[256]{0:T(256)}, u32[]{:S(2)}) copy-start(s32[256]{0:T(256)} %param.16) | copy-start | bytes 3076
  434.2 809.4 %all-gather.3.cloned.1.call-start = ((), (), s32[]{:S(2)}) async-start(), calls=%async_computation.1 | async-start | bytes 2162688 | tf_op jit(solution)/shard_map/all_gather | solution.py:357
  565.2 5.9 copy-start.5
  565.2 5.9 copy-start.17
  571.1 3.2 copy-start.21
  583.2 4.7 copy-start.22
  583.2 3.0 copy-start.24
  588.0 2.5 copy-start.26
  588.0 6.9 slice-start
  590.5 4.4 slice-start.1
  594.9 7.3 slice-start.2
  597.2 5.1 slice-start.3
  603.7 49.2 %copy-start.27 = (bf16[8,64,512]{2,1,0:T(8,128)(2,1)}, bf16[8,64,512]{2,1,0:T(8,128)(2,1)S(1)}, u32[]{:S(2)}) copy-start(bf16[8,64,512]{2,1,0:T(8,128)(2,1)S(1)} %fusion.35) | copy-start | bytes 1572868
  627.5 4.8 copy-start.9
  627.5 4.8 copy-start.44
  627.5 6.4 copy-start.8
  627.6 6.4 copy-start.43
  632.3 3.8 copy-start.41
  633.9 3.0 copy-start.62
  633.9 3.0 copy-start.66
  636.1 2.4 copy-start.50
  636.1 3.8 copy-start.38
  636.1 5.4 copy-start.18
  637.0 4.5 copy-start.7
  637.0 4.5 copy-start.13
  642.8 3.2 copy-start.34
  642.8 3.2 copy-start.46
  642.8 4.9 copy-start.23
  646.0 2.6 copy-start.14
  649.9 3.5 copy-start.32
  649.9 3.5 copy-start.64
  664.5 8.4 copy-start.30
  664.5 8.9 copy-start.29
  672.8 2.3 copy-start.31
  678.7 16.0 %copy-start.19 = (f32[512,512]{0,1:T(8,128)}, f32[512,512]{0,1:T(8,128)S(1)}, u32[]{:S(2)}) copy-start(f32[512,512]{0,1:T(8,128)S(1)} %convolution_add_fusion.2) | copy-start | bytes 3145732
  678.7 16.0 %copy-start.33 = (bf16[8,64,512]{2,1,0:T(8,128)(2,1)S(1)}, bf16[8,64,512]{2,1,0:T(8,128)(2,1)}, u32[]{:S(2)}) copy-start(bf16[8,64,512]{2,1,0:T(8,128)(2,1)} %fusion.38) | copy-start | bytes 1572868
  696.5 233.2 %copy-start.67 = (f32[512]{0:T(512)S(1)}, f32[512]{0:T(512)}, u32[]{:S(2)}) copy-start(f32[512]{0:T(512)} %get-tuple-element.109) | copy-start | bytes 6148
  696.5 233.3 %copy-start.68 = (f32[512]{0:T(512)S(1)}, f32[512]{0:T(512)}, u32[]{:S(2)}) copy-start(f32[512]{0:T(512)} %get-tuple-element.107) | copy-start | bytes 6148
  928.1 320.1 %all-gather.5.cloned.1.call-start = ((), (), s32[]{:S(2)}) async-start(), calls=%async_computation.2 | async-start | bytes 2162688 | tf_op jit(solution)/shard_map/all_gather | solution.py:360
  943.3 295.5 %all-to-all-start = ((bf16[32,2,4096]{2,1,0:T(2,128)(2,1)}), bf16[32,2,4096]{2,1,0:T(2,128)(2,1)S(1)}, u32[]{:S(2)}, u32[]{:S(2)}) async-start(bf16[32,2,4096]{2,1,0:T(2,128)(2,1)} %reshape.522), calls=%async_computation | async-start | bytes 1048576 | tf_op jit(solution)/shard_map/all_to_all | solution.py:340
  1243.6 9.3 copy-start.1
  (19 other events, 35.6 us)
Sparse Core Ops, SparseCore 0:
  434.3 122.9 all-reduce.13
  928.3 55.8 all-gather.2
  987.1 55.8 all-gather.4
